TPU v7x, 128 devices: a whole 4x4x4 slice. The times are simulated.
128 devices in a mesh: task: 8 (over x, core), param: 16 (over y, z).
Axes of the slice: x: 4, y: 4, z: 4, core: 2. Of those that a mesh axis runs over, the one named last changes fastest.
Arguments:
- acts: bfloat16 [128, 3584], replicated, may hold values from -6 to 6
- out_grads: bfloat16 [8, 128, 10240], P('task', None, 'param'), may hold values from -12 to 12
- order: int32 [8], replicated, may hold values from 0 to 7, each once
Outputs:
- update: float32 [3584, 10240], P('task', 'param')
- weights: float32 [8], replicated
All inputs are finite; a program needn't handle non-finite values.
Results may differ from a plain program's by a relative error of at most 0.0029.
Values may be sent and summed in bfloat16 or wider, within the bound.
No kernel may reach another device: no remote copies, remote signals or barrier semaphores. Data moves between devices by JAX's collectives and lax.ppermute only.
A program may use at most 64 MiB of HBM per device.

v0:
```python
import functools

import jax
import jax.numpy as jnp
from jax import lax
from jax.sharding import Mesh
from jax.sharding import PartitionSpec as P

TASK = ("task_0", "task_1")
TASK_PARAM = ("task_0", "task_1", "param_0", "param_1")
PARAM = ("param_0", "param_1")


def from_everyone(value, axis):
    devices = lax.axis_size(axis)
    return lax.all_to_all(
        jnp.broadcast_to(value[None], (devices, *value.shape)), axis, 0, 0, tiled=True
    )


def laid_out(blocks, dim):
    blocks = jnp.moveaxis(blocks, 0, dim)
    lengths = blocks.shape
    return blocks.reshape(*lengths[:dim], lengths[dim] * lengths[dim + 1], *lengths[dim + 2 :])


def collect(value, axis, dim):
    blocks = from_everyone(value, axis)
    return laid_out(blocks, dim)


def over_axes(value, axes):
    return functools.reduce(lax.psum, axes, value)


def task_grads(acts_part, blocks):
    return jnp.einsum("td,ktc->kdc", acts_part, blocks, preferred_element_type=jnp.float32).astype(
        jnp.bfloat16
    )


def pcgrad_weights(gram, order):
    count = gram.shape[0]
    ids = jnp.arange(count, dtype=jnp.int32)

    def turn(step, mix):
        target = order[step]
        column = gram[:, target]
        onehot = (ids == target).astype(jnp.float32)
        dots = jnp.dot(mix, column, precision=lax.Precision.HIGHEST)
        scale = jnp.sum(column * onehot) + 1e-06
        change = jnp.minimum(dots, 0.0) / scale * (1.0 - onehot)
        return mix - change[:, None] * onehot[None, :]

    mix = lax.fori_loop(0, count, turn, jnp.eye(count, dtype=jnp.float32))
    return jnp.sum(mix, axis=0)


def shards(acts, out_grads, order):
    local = out_grads.shape[0]
    groups = lax.axis_size(TASK)
    group_id = lax.axis_index(TASK)
    total_tasks = local * groups
    part_rows = acts.shape[1] // groups
    acts_rows = lax.dynamic_slice_in_dim(acts, group_id * part_rows, part_rows, 1)
    everyone = collect(out_grads, TASK, 0)
    row_grads = task_grads(acts_rows, everyone)
    flat = row_grads.reshape(total_tasks, -1)
    partial_gram = jnp.dot(flat, flat.T, preferred_element_type=jnp.float32)
    gram = over_axes(partial_gram, TASK_PARAM)
    weights = pcgrad_weights(gram, order)
    combined = jnp.einsum(
        "k,ktc->tc", weights, everyone.astype(jnp.float32), precision=lax.Precision.HIGHEST
    ).astype(jnp.bfloat16)
    update = lax.dot_general(
        acts_rows, combined, (((0,), (0,)), ((), ())), preferred_element_type=jnp.float32
    )
    return (update, weights)


def solution(mesh):
    split = Mesh(mesh.devices.reshape(4, 2, 4, 4), ("task_0", "task_1", "param_0", "param_1"))
    placed = (P(), P(TASK, None, PARAM), P())
    return jax.shard_map(
        shards, mesh=split, in_specs=placed, out_specs=(P(TASK, PARAM), P()), check_vma=False
    )
```

profile of v0, /device:TPU:0, one launch (start us, length us, event | category | flops | bytes accessed | tf_op | source)
XLA Modules:
  0.0 116.8 jit_solution(6982724442510270895)
XLA Ops:
  0.6 0.0 copy-start
  0.6 2.2 %broadcast_in_dim.15 = bf16[8,1,128,640]{3,2,1,0:T(8,128)(2,1)} broadcast(bf16[128,640]{1,0:T(8,128)(2,1)} %bitcast.41), dimensions={2,3} | broadcast | bytes 1474560 | tf_op jit(solution)/shard_map/broadcast_in_dim | solution.py:17
  2.8 4.4 %all-to-all-start = ((bf16[8,1,128,640]{3,2,1,0:T(8,128)(2,1)}), bf16[8,1,128,640]{3,2,1,0:T(8,128)(2,1)S(1)}, u32[]{:S(2)}, u32[]{:S(2)}) async-start(bf16[8,1,128,640]{3,2,1,0:T(8,128)(2,1)} %broadcast_in_dim.15), calls=%async_computation | async-start | bytes 2621440 | tf_op jit(solution)/shard_map/all_to_all | solution.py:16
  7.2 18.7 %all-to-all-done = bf16[8,1,128,640]{3,2,1,0:T(8,128)(2,1)S(1)} async-done(((bf16[8,1,128,640]{3,2,1,0:T(8,128)(2,1)}), bf16[8,1,128,640]{3,2,1,0:T(8,128)(2,1)S(1)}, u32[]{:S(2)}, u32[]{:S(2)}) %all-to-all-start) | async-done | bytes 1310752 | tf_op jit(solution)/shard_map/all_to_all | solution.py:16
  26.0 0.0 copy-done
  26.0 1.5 %fusion.15 = bf16[448,8,640]{2,0,1:T(8,128)(2,1)S(1)} fusion(bf16[128,3584]{1,0:T(8,128)(2,1)S(1)} %copy-done, s32[]{:T(128)S(6)} %select_n.15, bf16[8,1,128,640]{3,2,1,0:T(8,128)(2,1)S(1)} %all-to-all-done), kind=kOutput, calls=%fused_computation.18 | convolution fusion | flops 587202560 | bytes 6029316 | tf_op jit(solution)/shard_map/td,ktc->kdc/dot_general | solution.py:37
  27.4 0.0 copy-start.2
  27.5 3.8 %fusion.11 = f32[8,8]{1,0:T(8,128)S(1)} fusion(bf16[448,8,640]{2,0,1:T(8,128)(2,1)S(1)} %fusion.15), kind=kOutput, calls=%fused_computation.15 | convolution fusion | flops 36700160 | bytes 4587776 | tf_op jit(solution)/shard_map/dot_general | solution.py:69
  31.3 8.9 %psum.28 = f32[8,8]{1,0:T(8,128)S(1)} all-reduce(f32[8,8]{1,0:T(8,128)S(1)} %fusion.11), channel_id=1, replica_groups=mesh['task_0'=4,'task_1'=2,'param_0'=4,'param_1'=4] {'task_0'}, use_global_device_ids=true, to_apply=%region_0.0 | all-reduce | flops 64 | bytes 512 | tf_op jit(solution)/shard_map/psum | solution.py:33
  40.2 2.5 %psum.29 = f32[8,8]{1,0:T(8,128)S(1)} all-reduce(f32[8,8]{1,0:T(8,128)S(1)} %psum.28), channel_id=1, replica_groups=mesh['task_0'=4,'task_1'=2,'param_0'=4,'param_1'=4] {'task_1'}, use_global_device_ids=true, to_apply=%region_1.0 | all-reduce | flops 64 | bytes 512 | tf_op jit(solution)/shard_map/psum | solution.py:33
  42.6 10.7 %psum.30 = f32[8,8]{1,0:T(8,128)S(1)} all-reduce(f32[8,8]{1,0:T(8,128)S(1)} %psum.29), channel_id=1, replica_groups=mesh['task_0'=4,'task_1'=2,'param_0'=4,'param_1'=4] {'param_0'}, use_global_device_ids=true, to_apply=%region_2.0 | all-reduce | flops 64 | bytes 512 | tf_op jit(solution)/shard_map/psum | solution.py:33
  53.3 11.8 %psum.31 = f32[8,8]{1,0:T(8,128)S(1)} all-reduce(f32[8,8]{1,0:T(8,128)S(1)} %psum.30), channel_id=1, replica_groups=mesh['task_0'=4,'task_1'=2,'param_0'=4,'param_1'=4] {'param_1'}, use_global_device_ids=true, to_apply=%region_3.0 | all-reduce | flops 64 | bytes 512 | tf_op jit(solution)/shard_map/psum | solution.py:33
  65.1 0.1 copy.5
  65.2 0.0 copy-done.2
  65.2 48.5 %while.14 = (s32[]{:T(128)}, f32[8,8]{1,0:T(8,128)S(1)}, s32[8]{0:T(128)S(1)}, f32[8,8]{0,1:T(8,128)S(1)}, s32[]{:T(128)}, /*index=5*/s32[]{:T(128)}, s32[]{:T(128)}, f32[]{:T(128)}) while((s32[]{:T(128)}, f32[8,8]{1,0:T(8,128)S(1)}, s32[8]{0:T(128)S(1)}, f32[8,8]{0,1:T(8,128)S(1)}, s32[]{:T(128)}, /*index=5*/s32[]{:T(128)}, ...), condition=%wide.region_6.0_spmd.clone, body=%wide.region_4.0_spmd.clone.sunk | while | flops 989 | bytes 5451 | solution.py:55
  65.2 0.6 dynamic_slice.35
  67.7 1.3 %fusion.29 = f32[]{:T(128)} fusion(s32[]{:T(128)} %bitcast.39, f32[8,8]{0,1:T(8,128)S(1)} %get-tuple-element.163, s32[]{:T(128)S(6)} %select_n.18), kind=kLoop, calls=%fused_computation.8.clone.1 | loop fusion | flops 23 | bytes 44 | tf_op jit(solution)/shard_map/while/body/eval_jaxpr/reduce_sum | solution.py:51
  69.7 0.8 fusion.30
  70.5 0.7 compare_convert_fusion.2
  71.2 0.1 multiply_subtract_fusion.2
  71.2 0.6 dynamic_slice.35
  73.8 1.3 %fusion.29 = f32[]{:T(128)} fusion(s32[]{:T(128)} %bitcast.39, f32[8,8]{0,1:T(8,128)S(1)} %get-tuple-element.163, s32[]{:T(128)S(6)} %select_n.18), kind=kLoop, calls=%fused_computation.8.clone.1 | loop fusion | flops 23 | bytes 44 | tf_op jit(solution)/shard_map/while/body/eval_jaxpr/reduce_sum | solution.py:51
  75.8 0.8 fusion.30
  76.6 0.7 compare_convert_fusion.2
  77.2 0.1 multiply_subtract_fusion.2
  77.3 0.6 dynamic_slice.35
  79.8 1.3 %fusion.29 = f32[]{:T(128)} fusion(s32[]{:T(128)} %bitcast.39, f32[8,8]{0,1:T(8,128)S(1)} %get-tuple-element.163, s32[]{:T(128)S(6)} %select_n.18), kind=kLoop, calls=%fused_computation.8.clone.1 | loop fusion | flops 23 | bytes 44 | tf_op jit(solution)/shard_map/while/body/eval_jaxpr/reduce_sum | solution.py:51
  81.9 0.8 fusion.30
  82.6 0.7 compare_convert_fusion.2
  83.3 0.1 multiply_subtract_fusion.2
  83.4 0.6 dynamic_slice.35
  85.9 1.3 %fusion.29 = f32[]{:T(128)} fusion(s32[]{:T(128)} %bitcast.39, f32[8,8]{0,1:T(8,128)S(1)} %get-tuple-element.163, s32[]{:T(128)S(6)} %select_n.18), kind=kLoop, calls=%fused_computation.8.clone.1 | loop fusion | flops 23 | bytes 44 | tf_op jit(solution)/shard_map/while/body/eval_jaxpr/reduce_sum | solution.py:51
  87.9 0.8 fusion.30
  88.7 0.7 compare_convert_fusion.2
  89.4 0.1 multiply_subtract_fusion.2
  89.4 0.6 dynamic_slice.35
  92.0 1.3 %fusion.29 = f32[]{:T(128)} fusion(s32[]{:T(128)} %bitcast.39, f32[8,8]{0,1:T(8,128)S(1)} %get-tuple-element.163, s32[]{:T(128)S(6)} %select_n.18), kind=kLoop, calls=%fused_computation.8.clone.1 | loop fusion | flops 23 | bytes 44 | tf_op jit(solution)/shard_map/while/body/eval_jaxpr/reduce_sum | solution.py:51
  94.0 0.8 fusion.30
  94.8 0.7 compare_convert_fusion.2
  95.4 0.1 multiply_subtract_fusion.2
  95.5 0.6 dynamic_slice.35
  98.0 1.3 %fusion.29 = f32[]{:T(128)} fusion(s32[]{:T(128)} %bitcast.39, f32[8,8]{0,1:T(8,128)S(1)} %get-tuple-element.163, s32[]{:T(128)S(6)} %select_n.18), kind=kLoop, calls=%fused_computation.8.clone.1 | loop fusion | flops 23 | bytes 44 | tf_op jit(solution)/shard_map/while/body/eval_jaxpr/reduce_sum | solution.py:51
  100.1 0.8 fusion.30
  100.8 0.7 compare_convert_fusion.2
  101.5 0.1 multiply_subtract_fusion.2
  101.6 0.6 dynamic_slice.35
  104.1 1.3 %fusion.29 = f32[]{:T(128)} fusion(s32[]{:T(128)} %bitcast.39, f32[8,8]{0,1:T(8,128)S(1)} %get-tuple-element.163, s32[]{:T(128)S(6)} %select_n.18), kind=kLoop, calls=%fused_computation.8.clone.1 | loop fusion | flops 23 | bytes 44 | tf_op jit(solution)/shard_map/while/body/eval_jaxpr/reduce_sum | solution.py:51
  106.1 0.8 fusion.30
  106.9 0.7 compare_convert_fusion.2
  107.6 0.1 multiply_subtract_fusion.2
  107.7 0.6 dynamic_slice.35
  110.2 1.3 %fusion.29 = f32[]{:T(128)} fusion(s32[]{:T(128)} %bitcast.39, f32[8,8]{0,1:T(8,128)S(1)} %get-tuple-element.163, s32[]{:T(128)S(6)} %select_n.18), kind=kLoop, calls=%fused_computation.8.clone.1 | loop fusion | flops 23 | bytes 44 | tf_op jit(solution)/shard_map/while/body/eval_jaxpr/reduce_sum | solution.py:51
  112.2 0.8 fusion.30
  113.0 0.7 compare_convert_fusion.2
  113.7 0.1 multiply_subtract_fusion.2
  113.7 0.0 copy-start.1
  113.7 1.6 %fusion.9 = bf16[1,128,640]{2,0,1:T(2,128)(2,1)S(1)} fusion(bf16[8,128,640]{2,1,0:T(8,128)(2,1)S(1)} %bitcast.40, f32[8]{0:T(128)S(1)} %reduce_sum.22), kind=kOutput, calls=%fused_computation.13 | convolution fusion | flops 7864320 | bytes 1474592 | tf_op jit(solution)/shard_map/k,ktc->tc/dot_general | solution.py:72
  115.4 1.4 %fusion.14 = f32[448,640]{1,0:T(8,128)} fusion(bf16[1,128,640]{2,0,1:T(2,128)(2,1)S(1)} %fusion.9, bf16[128,3584]{1,0:T(8,128)(2,1)S(1)} %copy-done, s32[]{:T(128)S(6)} %select_n.15), kind=kOutput, calls=%fused_computation.17 | convolution fusion | flops 73400320 | bytes 1605636 | tf_op jit(solution)/shard_map/dot_general | solution.py:75
  116.8 0.0 copy-done.1
  (2 shorter events, 0.0 us)
Async XLA Ops:
  0.6 25.3 %copy-start = (bf16[128,3584]{1,0:T(8,128)(2,1)S(1)}, bf16[128,3584]{1,0:T(8,128)(2,1)}, u32[]{:S(2)}) copy-start(bf16[128,3584]{1,0:T(8,128)(2,1)} %param.5) | copy-start | bytes 2752516
  2.8 23.2 %all-to-all-start = ((bf16[8,1,128,640]{3,2,1,0:T(8,128)(2,1)}), bf16[8,1,128,640]{3,2,1,0:T(8,128)(2,1)S(1)}, u32[]{:S(2)}, u32[]{:S(2)}) async-start(bf16[8,1,128,640]{3,2,1,0:T(8,128)(2,1)} %broadcast_in_dim.15), calls=%async_computation | async-start | bytes 2621440 | tf_op jit(solution)/shard_map/all_to_all | solution.py:16
  27.4 37.7 %copy-start.2 = (s32[8]{0:T(128)S(1)}, s32[8]{0:T(128)}, u32[]{:S(2)}) copy-start(s32[8]{0:T(128)} %param.7) | copy-start | bytes 100
  113.7 3.0 %copy-start.1 = (f32[8]{0:T(128)}, f32[8]{0:T(128)S(1)}, u32[]{:S(2)}) copy-start(f32[8]{0:T(128)S(1)} %reduce_sum.22) | copy-start | bytes 100
where the time goes:
time: 118 us; the launch traced here: 117 us
  blocking collectives  33.8 us (29%)
  loops' own time  21.2 us (18%)
  waiting for transfers between devices  18.7 us (16%)
  other arithmetic  16.5 us (14%)
  matrix products  14.6 us (12%)
  local copies, waits for them, and re-layouts  6.92 us (6%)
  starting transfers between devices  4.41 us (4%)
    psum x4, blocking collectives, over_axes(): return functools.reduce(lax.psum, axes, value)  33.8 us
    another operation x1, loops' own time, pcgrad_weights(): mix = lax.fori_loop(0, count, turn, jnp.eye(count, dtype=jnp.float32))  21.2 us
    all_to_all x1, waiting for transfers between devices, from_everyone(): lax.all_to_all(jnp.broadcast_to(value[None], (devices, *value.shape)), ax...  18.7 us
    reduce_sum x8, other arithmetic, turn(): scale = jnp.sum(column * onehot) + 1e-06  10.6 us
    dot_general x8, matrix products, turn(): dots = jnp.dot(mix, column, precision=lax.Precision.HIGHEST)  6.24 us
    convert_element_type x8, other arithmetic, turn(): onehot = (ids == target).astype(jnp.float32)  5.25 us
    dynamic_slice x8, local copies, waits for them, and re-layouts, turn(): target = order[step]  4.66 us
    all_to_all x1, starting transfers between devices, from_everyone(): lax.all_to_all(jnp.broadcast_to(value[None], (devices, *value.shape)), ax...  4.41 us
  transfers between devices with their start and end apart: 1, of which 1 were waited for; matrix products, arithmetic and copies ran while one was open for 0% of the time, Pallas kernels for 0%

commit v1 on v0

v1 whole, which is shorter than its diff:
```python
import functools

import jax
import jax.numpy as jnp
from jax import lax
from jax.experimental import pallas as pl
from jax.experimental.pallas import tpu as pltpu
from jax.sharding import Mesh
from jax.sharding import PartitionSpec as P

TASK = ("task_0", "task_1")
PARAM = ("param_0", "param_1")
LANES = 128


def from_everyone(value, axis):
    devices = lax.axis_size(axis)
    return lax.all_to_all(
        jnp.broadcast_to(value[None], (devices, *value.shape)), axis, 0, 0, tiled=True
    )


def gram_kernel(mine_ref, other_ref, outer_ref, gram_ref, all_ref, rows_ref):
    core = lax.axis_index("task_1")
    chips, tokens, _ = mine_ref.shape
    tasks = 2 * chips
    for chip in range(chips):
        all_ref[pl.ds(2 * chip + core, 1)] = mine_ref[chip : chip + 1]
        all_ref[pl.ds(2 * chip + 1 - core, 1)] = other_ref[chip : chip + 1]
    outer = outer_ref[...]
    for i in range(tasks):
        for j in range(i, tasks):
            pair = lax.dot_general(
                all_ref[i], all_ref[j], (((1,), (1,)), ((), ())), preferred_element_type=jnp.float32
            )
            row = jnp.sum(pair * outer, axis=0, keepdims=True)
            rows_ref[j, i : i + 1, :] = row
            if j > i:
                rows_ref[i, j : j + 1, :] = row
    lane = lax.broadcasted_iota(jnp.int32, (tasks, LANES), 1)
    gram = jnp.zeros((tasks, LANES), jnp.float32)
    for j in range(tasks):
        gram = jnp.where(lane == j, jnp.sum(rows_ref[j], axis=1, keepdims=True), gram)
    gram_ref[...] = gram


def partial_gram(mine, other, outer):
    chips, tokens, width = mine.shape
    tasks = 2 * chips
    flops = tasks * (tasks + 1) * tokens * tokens * width
    return pl.pallas_call(
        gram_kernel,
        out_shape=jax.ShapeDtypeStruct((tasks, LANES), jnp.float32),
        in_specs=[pl.BlockSpec(memory_space=pltpu.VMEM)] * 3,
        out_specs=pl.BlockSpec(memory_space=pltpu.VMEM),
        scratch_shapes=[
            pltpu.VMEM((tasks, tokens, width), jnp.bfloat16),
            pltpu.VMEM((tasks, tasks, LANES), jnp.float32),
        ],
        cost_estimate=pl.CostEstimate(flops=flops, bytes_accessed=0, transcendentals=0),
        compiler_params=pltpu.CompilerParams(vmem_limit_bytes=12 << 20),
        name="partial_gram",
    )(mine, other, outer)


def finish_kernel(
    order_ref, grams_ref, mine_ref, other_ref, acts_ref, update_ref, weights_ref,
    columns_ref, scales_ref, spread_ref, out_ref, sems,
):
    core = lax.axis_index("task_1")
    chips, tokens, width = mine_ref.shape
    tasks = 2 * chips
    lane = lax.broadcasted_iota(jnp.int32, (tasks, LANES), 1)
    sub = lax.broadcasted_iota(jnp.int32, (tasks, LANES), 0)
    gram = grams_ref[0]
    for k in range(1, grams_ref.shape[0]):
        gram = gram + grams_ref[k]
    for j in range(tasks):
        column = jnp.sum(jnp.where(lane == j, gram, 0.0), axis=1, keepdims=True)
        columns_ref[j] = jnp.broadcast_to(column, (tasks, LANES))
        scales_ref[j] = jnp.broadcast_to(column[j : j + 1], (tasks, LANES)) + 1e-06
    mix = (lane == sub).astype(jnp.float32)
    for step in range(tasks):
        target = order_ref[step]
        dots = jnp.sum(mix * columns_ref[target], axis=0, keepdims=True)
        change = jnp.minimum(dots, 0.0) / scales_ref[target]
        mix = mix - jnp.where((sub == target) & (lane != target), change, 0.0)
    weights = jnp.sum(jnp.where(lane < tasks, mix, 0.0), axis=1, keepdims=True)
    spread = jnp.broadcast_to(weights, (tasks, LANES))
    spread_ref[...] = spread
    weights_ref[...] = jnp.sum(jnp.where(lane == sub, spread, 0.0), axis=0, keepdims=True)
    factors = []
    for chip in range(chips):
        factors.append(spread_ref[pl.ds(2 * chip, 1), :])
        factors.append(spread_ref[pl.ds(2 * chip + 1, 1), :])
    copies = []
    for block in range(width // LANES):
        cols = pl.ds(block * LANES, LANES)
        total = jnp.zeros((tokens, LANES), jnp.float32)
        for chip in range(chips):
            a = mine_ref[chip, :, cols]
            b = other_ref[chip, :, cols]
            first = jnp.where(core == 0, a, b).astype(jnp.float32)
            second = jnp.where(core == 0, b, a).astype(jnp.float32)
            total = total + factors[2 * chip] * first
            total = total + factors[2 * chip + 1] * second
        out_ref[:, cols] = lax.dot_general(
            acts_ref[...], total.astype(jnp.bfloat16), (((1,), (0,)), ((), ())),
            preferred_element_type=jnp.float32,
        )
        copy = pltpu.make_async_copy(out_ref.at[:, cols], update_ref.at[:, cols], sems.at[block])
        copy.start()
        copies.append(copy)
    for copy in copies:
        copy.wait()


def finish(order, grams, mine, other, acts_rows):
    chips, tokens, width = mine.shape
    tasks = 2 * chips
    rows = acts_rows.shape[0]
    vmem = pl.BlockSpec(memory_space=pltpu.VMEM)
    return pl.pallas_call(
        finish_kernel,
        out_shape=(
            jax.ShapeDtypeStruct((rows, width), jnp.float32),
            jax.ShapeDtypeStruct((1, LANES), jnp.float32),
        ),
        in_specs=[pl.BlockSpec(memory_space=pltpu.SMEM), vmem, vmem, vmem, vmem],
        out_specs=(pl.BlockSpec(memory_space=pl.ANY), vmem),
        scratch_shapes=[
            pltpu.VMEM((tasks, tasks, LANES), jnp.float32),
            pltpu.VMEM((tasks, tasks, LANES), jnp.float32),
            pltpu.VMEM((tasks, LANES), jnp.float32),
            pltpu.VMEM((rows, width), jnp.float32),
            pltpu.SemaphoreType.DMA((width // LANES,)),
        ],
        cost_estimate=pl.CostEstimate(
            flops=2 * rows * tokens * width, bytes_accessed=4 * rows * width, transcendentals=0
        ),
        compiler_params=pltpu.CompilerParams(vmem_limit_bytes=12 << 20),
        name="finish",
    )(order, grams, mine, other, acts_rows)


def shards(acts, out_grads, order):
    groups = lax.axis_size(TASK)
    group_id = lax.axis_index(TASK)
    part_rows = acts.shape[1] // groups
    mine = from_everyone(out_grads[0], "task_0")
    outer = lax.dot_general(acts, acts, (((1,), (1,)), ((), ())), preferred_element_type=jnp.float32)
    acts_rows = lax.dynamic_slice_in_dim(acts, group_id * part_rows, part_rows, 1).T
    other = lax.ppermute(mine, "task_1", [(0, 1), (1, 0)])
    grams = from_everyone(partial_gram(mine, other, outer), PARAM)
    update, weights = finish(order, grams, mine, other, acts_rows)
    return (update, weights[0, :groups])


def solution(mesh):
    split = Mesh(mesh.devices.reshape(4, 2, 4, 4), ("task_0", "task_1", "param_0", "param_1"))
    placed = (P(), P(TASK, None, PARAM), P())
    return jax.shard_map(
        shards, mesh=split, in_specs=placed, out_specs=(P(TASK, PARAM), P()), check_vma=False
    )
```

time: 118 us -> 40.7 us (0.34)
  loops' own time: 21.2 us -> 0 us
  blocking collectives: 33.8 us -> 15.1 us
  other arithmetic: 16.5 us -> 0 us
  matrix products: 14.6 us -> 0.39 us
  waiting for transfers between devices: 18.7 us -> 9.09 us
  Pallas kernels: 0 us -> 4.67 us
  local copies, waits for them, and re-layouts: 6.92 us -> 2.47 us
  starting transfers between devices: 4.41 us -> 8.05 us
    psum x4 -> x0, blocking collectives: 33.8 us -> none  [over_axes(): return functools.reduce(lax.psum, axes, value)]
    another operation x1 -> x0, loops' own time: 21.2 us -> none  [pcgrad_weights(): mix = lax.fori_loop(0, count, turn, jnp.eye(count, dtype=jnp.float32))]
    all_to_all x0 -> x1, blocking collectives: none -> 15.1 us  [from_everyone(): lax.all_to_all(jnp.broadcast_to(value[None], (devices, *value.shape)), ax...]
    dot_general x12 -> x1, matrix products: 14.6 us -> 0.39 us  [shards(): lax.dot_general(acts, acts, (((1,), (1,)), ((), ())), preferred_element_t...]
    all_to_all x1, waiting for transfers between devices: 18.7 us -> 7.41 us  [from_everyone(): lax.all_to_all(jnp.broadcast_to(value[None], (devices, *value.shape)), ax...]
    reduce_sum x9 -> x0, other arithmetic: 10.6 us -> none  [the longest x8 10.6 us: turn(): scale = jnp.sum(column * onehot) + 1e-06]
    convert_element_type x9 -> x0, other arithmetic: 5.25 us -> none  [the longest x8 5.25 us: turn(): onehot = (ids == target).astype(jnp.float32)]
    pallas_call x0 -> x2, Pallas kernels: none -> 4.67 us  [the longest x1 2.48 us: partial_gram(): pl.pallas_call(gram_kernel, out_shape=jax.ShapeDtypeStruct((tasks, LANES)...]
  transfers between devices with their start and end apart: 1 -> 2, of which waited for: 1 -> 2; matrix products, arithmetic and copies ran while one was open for 0% -> 2% of each run, Pallas kernels for 0% -> 0%
where the time goes in v1:
time: 40.7 us; the launch traced here: 40.4 us
  blocking collectives  15.1 us (37%)
  waiting for transfers between devices  9.09 us (22%)
  starting transfers between devices  8.05 us (20%)
  Pallas kernels  4.67 us (11%)
  local copies, waits for them, and re-layouts  2.47 us (6%)
  between operations  0.68 us (2%)
    all_to_all x1, blocking collectives, from_everyone(): lax.all_to_all(jnp.broadcast_to(value[None], (devices, *value.shape)), ax...  15.1 us
    all_to_all x1, starting transfers between devices, from_everyone(): lax.all_to_all(jnp.broadcast_to(value[None], (devices, *value.shape)), ax...  8.05 us
    all_to_all x1, waiting for transfers between devices, from_everyone(): lax.all_to_all(jnp.broadcast_to(value[None], (devices, *value.shape)), ax...  7.41 us
    pallas_call x1, Pallas kernels, partial_gram(): pl.pallas_call(gram_kernel, out_shape=jax.ShapeDtypeStruct((tasks, LANES)...  2.48 us
    pallas_call x1, Pallas kernels, finish(): pl.pallas_call(finish_kernel, out_shape=(jax.ShapeDtypeStruct((rows, widt...  2.18 us
    broadcast_in_dim x2, local copies, waits for them, and re-layouts, from_everyone(): jnp.broadcast_to(value[None], (devices, *value.shape))  1.69 us
    ppermute x1, waiting for transfers between devices, shards(): other = lax.ppermute(mine, 'task_1', [(0, 1), (1, 0)])  1.68 us
  transfers between devices with their start and end apart: 2, of which 2 were waited for; matrix products, arithmetic and copies ran while one was open for 2% of the time, Pallas kernels for 0%

profile of v1, /device:TPU:0, one launch (start us, length us, event | category | flops | bytes accessed | tf_op | source)
XLA Modules:
  0.0 40.4 jit_solution(13193143587417511362)
XLA Ops:
  0.6 0.0 copy-start
  0.6 1.0 %broadcast_in_dim.14 = bf16[4,128,640]{2,1,0:T(8,128)(2,1)S(1)} broadcast(bf16[128,640]{1,0:T(8,128)(2,1)} %bitcast.7), dimensions={1,2} | broadcast | bytes 819200 | tf_op jit(solution)/shard_map/broadcast_in_dim | solution.py:19
  1.7 15.1 %all_to_all.10.mine_ref = bf16[4,128,640]{2,1,0:T(8,128)(2,1)S(1)} all-to-all(bf16[4,128,640]{2,1,0:T(8,128)(2,1)S(1)} %broadcast_in_dim.14), channel_id=1, replica_groups=mesh['task_0'=4,'task_1'=2,'param_0'=4,'param_1'=4] {'task_0'}, dimensions={0} | all-to-all | bytes 1310720 | tf_op jit(solution)/shard_map/all_to_all | solution.py:18
  16.8 0.0 collective-permute-start
  16.8 0.0 copy-done
  16.8 0.4 fusion.outer_ref
  17.2 0.0 copy-start.1
  17.2 1.7 %collective-permute-done.other_ref = bf16[4,128,640]{2,1,0:T(8,128)(2,1)S(1)} collective-permute-done((bf16[4,128,640]{2,1,0:T(8,128)(2,1)S(1)}, bf16[4,128,640]{2,1,0:T(8,128)(2,1)S(1)}, u32[]{:S(2)}, u32[]{:S(2)}) %collective-permute-start) | collective-permute-done | bytes 655392 | tf_op jit(solution)/shard_map/ppermute | solution.py:153
  18.9 2.5 %partial_gram.1 = f32[8,128]{1,0:T(8,128)S(1)} custom-call(bf16[4,128,640]{2,1,0:T(8,128)(2,1)S(1)} %all_to_all.10.mine_ref, bf16[4,128,640]{2,1,0:T(8,128)(2,1)S(1)} %collective-permute-done.other_ref, f32[128,128]{1,0:T(8,128)S(1)} %fusion.outer_ref), custom_call_target="tpu_custom_call" | custom-call | flops 754974720 | tf_op jit(solution)/shard_map/partial_gram/pallas_call | solution.py:51
  21.4 0.6 %broadcast_in_dim.15 = f32[16,8,128]{2,1,0:T(8,128)} broadcast(f32[8,128]{1,0:T(8,128)S(1)} %partial_gram.1), dimensions={1,2} | broadcast | bytes 69632 | tf_op jit(solution)/shard_map/broadcast_in_dim | solution.py:19
  22.0 8.0 %all-to-all-start.1 = ((f32[16,8,128]{2,1,0:T(8,128)}), f32[16,8,128]{2,1,0:T(8,128)S(1)}, u32[]{:S(2)}, u32[]{:S(2)}) async-start(f32[16,8,128]{2,1,0:T(8,128)} %broadcast_in_dim.15), calls=%async_computation.1 | async-start | bytes 131072 | tf_op jit(solution)/shard_map/all_to_all | solution.py:18
  30.1 0.1 constant_dynamic-slice_fusion
  30.2 0.1 copy.6
  30.3 7.4 %all-to-all-done.1.grams_ref = f32[16,8,128]{2,1,0:T(8,128)S(1)} async-done(((f32[16,8,128]{2,1,0:T(8,128)}), f32[16,8,128]{2,1,0:T(8,128)S(1)}, u32[]{:S(2)}, u32[]{:S(2)}) %all-to-all-start.1) | async-done | bytes 65568 | tf_op jit(solution)/shard_map/all_to_all | solution.py:18
  37.7 0.0 copy-done.1
  37.7 2.2 %finish.1 = (f32[448,640]{1,0:T(8,128)}, f32[1,128]{1,0:T(1,128)S(1)}) custom-call(s32[8]{0:T(128)S(1)} %copy-done.1, f32[16,8,128]{2,1,0:T(8,128)S(1)} %all-to-all-done.1.grams_ref, bf16[4,128,640]{2,1,0:T(8,128)(2,1)S(1)} %all_to_all.10.mine_ref, bf16[4,128,640]{2,1,0:T(8,128)(2,1)S(1)} %collective-permute-done.other_ref, bf16[448,128]{1,0:T(8,128)(2,1)S(1)} %bitcast.6), custom_call_target="tpu_custom_call" | custom-call | flops 73400320 | bytes 1146880 | tf_op jit(solution)/shard_map/finish/pallas_call | solution.py:123
  39.9 0.5 %slice_bitcast_fusion = f32[8]{0:T(128)} fusion(f32[1,128]{1,0:T(1,128)S(1)} %get-tuple-element.5), kind=kLoop, calls=%fused_computation | loop fusion | bytes 64 | tf_op jit(solution)/shard_map/squeeze | solution.py:156
Async XLA Ops:
  0.6 16.2 %copy-start = (bf16[128,3584]{1,0:T(8,128)(2,1)S(1)}, bf16[128,3584]{1,0:T(8,128)(2,1)}, u32[]{:S(2)}) copy-start(bf16[128,3584]{1,0:T(8,128)(2,1)} %param.3) | copy-start | bytes 2752516
  16.8 2.1 %collective-permute-start = (bf16[4,128,640]{2,1,0:T(8,128)(2,1)S(1)}, bf16[4,128,640]{2,1,0:T(8,128)(2,1)S(1)}, u32[]{:S(2)}, u32[]{:S(2)}) collective-permute-start(bf16[4,128,640]{2,1,0:T(8,128)(2,1)S(1)} %all_to_all.10.mine_ref), channel_id=1, source_target_pairs={{0,16},{16,0},{1,17},{17,1},{2,18},{18,2},{3,19},{19,3},{4,20},{20... | collective-permute-start | bytes 1966088 | tf_op jit(solution)/shard_map/ppermute | solution.py:153
  17.2 20.5 %copy-start.1 = (s32[8]{0:T(128)S(1)}, s32[8]{0:T(128)}, u32[]{:S(2)}) copy-start(s32[8]{0:T(128)} %order_ref.1) | copy-start | bytes 100
  22.0 15.7 %all-to-all-start.1 = ((f32[16,8,128]{2,1,0:T(8,128)}), f32[16,8,128]{2,1,0:T(8,128)S(1)}, u32[]{:S(2)}, u32[]{:S(2)}) async-start(f32[16,8,128]{2,1,0:T(8,128)} %broadcast_in_dim.15), calls=%async_computation.1 | async-start | bytes 131072 | tf_op jit(solution)/shard_map/all_to_all | solution.py:18

commit v2 on v1

v2 whole, which is shorter than its diff:
```python
import jax
import jax.numpy as jnp
from jax import lax
from jax.experimental import pallas as pl
from jax.experimental.pallas import tpu as pltpu
from jax.sharding import Mesh
from jax.sharding import PartitionSpec as P

TASK = ("task_0", "task_1")
PARAM = ("param_0", "param_1")
LANES = 128
VMEM = pl.BlockSpec(memory_space=pltpu.VMEM)


def params(mib):
    return pltpu.CompilerParams(vmem_limit_bytes=mib << 20)


def chip_at(offset, chips):
    return lax.rem(lax.axis_index("task_0") + offset, chips)


def gram_kernel(*refs):
    chips = (len(refs) - 4) // 2
    mine, other = refs[:chips], refs[chips : 2 * chips]
    outer_ref, row_ref, flat_ref, rows_ref = refs[2 * chips :]
    core = lax.axis_index("task_1")
    tokens = outer_ref.shape[0]
    tasks = 2 * chips
    for offset in range(chips):
        base = chip_at(offset, chips) * 2
        flat_ref[base + core] = mine[offset][...]
        flat_ref[base + 1 - core] = other[offset][...]
    outer = outer_ref[...]
    for i in range(0, tasks, 2):
        for j in range(i, tasks, 2):
            block = lax.dot_general(
                flat_ref[i : i + 2].reshape(2 * tokens, -1), flat_ref[j : j + 2].reshape(2 * tokens, -1),
                (((1,), (1,)), ((), ())), preferred_element_type=jnp.float32,
            )
            for a in range(2):
                for b in range(2):
                    p, q = i + a, j + b
                    if q < p:
                        continue
                    pair = block[tokens * a : tokens * (a + 1), tokens * b : tokens * (b + 1)]
                    row = jnp.sum(pair * outer, axis=0, keepdims=True)
                    rows_ref[q, p : p + 1, :] = row
                    if q > p:
                        rows_ref[p, q : q + 1, :] = row
    lane = lax.broadcasted_iota(jnp.int32, (tasks, LANES), 1)
    sub = lax.broadcasted_iota(jnp.int32, (tasks, LANES), 0)
    gram = jnp.zeros((tasks, LANES), jnp.float32)
    for j in range(tasks):
        total = jnp.sum(rows_ref[j], axis=1, keepdims=True)
        gram = jnp.where(lane == tasks * sub + j, total, gram)
    row_ref[...] = jnp.broadcast_to(jnp.sum(gram, axis=0, keepdims=True), row_ref.shape)


def partial_gram(mine, other, outer, copies):
    tokens, width = mine[0].shape
    tasks = 2 * len(mine)
    flops = tasks * tasks * tokens * tokens * width
    return pl.pallas_call(
        gram_kernel,
        out_shape=jax.ShapeDtypeStruct((copies, LANES), jnp.float32),
        in_specs=[VMEM] * (tasks + 1),
        out_specs=VMEM,
        scratch_shapes=[
            pltpu.VMEM((tasks, tokens, width), jnp.bfloat16),
            pltpu.VMEM((tasks, tasks, LANES), jnp.float32),
        ],
        compiler_params=params(8),
        cost_estimate=pl.CostEstimate(flops=flops, bytes_accessed=0, transcendentals=0),
        name="partial_gram",
    )(*mine, *other, outer)


def finish_kernel(*refs):
    chips = (len(refs) - 9) // 2
    order_ref, grams_ref = refs[:2]
    mine, other = refs[2 : 2 + chips], refs[2 + chips : 2 + 2 * chips]
    acts_ref, update_ref, weights_ref, columns_ref, factor_ref, spread_ref, out_ref, sems = refs[-8:]
    core = lax.axis_index("task_1")
    tokens, width = mine[0].shape
    tasks = 2 * chips
    lane = lax.broadcasted_iota(jnp.int32, (tasks, LANES), 1)
    sub = lax.broadcasted_iota(jnp.int32, (tasks, LANES), 0)
    gram = jnp.sum(grams_ref[...], axis=0, keepdims=True)
    gram = jnp.where((lane >= tasks * sub) & (lane < tasks * sub + tasks), gram, 0.0)
    column_of = lane - tasks * sub
    diagonal = jnp.sum(jnp.where(column_of == sub, gram, 0.0), axis=1, keepdims=True)
    factor_ref[...] = 1.0 / (jnp.broadcast_to(diagonal, (tasks, LANES)) + 1e-06)
    for j in range(tasks):
        column = jnp.sum(jnp.where(column_of == j, gram, 0.0), axis=1, keepdims=True)
        columns_ref[j] = jnp.broadcast_to(column, (tasks, LANES))
    mix = (lane == sub).astype(jnp.float32)
    for step in range(tasks):
        target = order_ref[step]
        dots = jnp.sum(mix * columns_ref[target], axis=0, keepdims=True)
        change = jnp.minimum(dots, 0.0) * factor_ref[pl.ds(target, 1), :]
        mix = mix - jnp.where((sub == target) & (lane != target), change, 0.0)
    weights = jnp.sum(jnp.where(lane < tasks, mix, 0.0), axis=1, keepdims=True)
    spread = jnp.broadcast_to(weights, (tasks, LANES))
    spread_ref[...] = spread
    weights_ref[...] = jnp.sum(jnp.where(lane == sub, spread, 0.0), axis=0)[:tasks]
    terms = []
    for offset in range(chips):
        base = chip_at(offset, chips) * 2
        terms.append((spread_ref[pl.ds(base + core, 1), :], mine[offset]))
        terms.append((spread_ref[pl.ds(base + 1 - core, 1), :], other[offset]))
    copies = []
    for start in range(0, width, 256):
        size = min(256, width - start)
        blocks = []
        for at in range(start, start + size, LANES):
            total = None
            for factor, ref in terms:
                part = factor * ref[:, at : at + LANES].astype(jnp.float32)
                total = part if total is None else total + part
            blocks.append(total.astype(jnp.bfloat16))
        cols = pl.ds(start, size)
        out_ref[:, cols] = lax.dot_general(
            acts_ref[...], jnp.concatenate(blocks, axis=1), (((1,), (0,)), ((), ())),
            preferred_element_type=jnp.float32,
        )
        copy = pltpu.make_async_copy(out_ref.at[:, cols], update_ref.at[:, cols], sems.at[len(copies)])
        copy.start()
        copies.append(copy)
    for copy in copies:
        copy.wait()


def finish(order, grams, mine, other, acts_rows):
    tokens, width = mine[0].shape
    tasks = 2 * len(mine)
    rows = acts_rows.shape[0]
    return pl.pallas_call(
        finish_kernel,
        out_shape=(
            jax.ShapeDtypeStruct((rows, width), jnp.float32),
            jax.ShapeDtypeStruct((tasks,), jnp.float32),
        ),
        in_specs=[pl.BlockSpec(memory_space=pltpu.SMEM)] + [VMEM] * (tasks + 2),
        out_specs=(pl.BlockSpec(memory_space=pl.ANY), VMEM),
        scratch_shapes=[
            pltpu.VMEM((tasks, tasks, LANES), jnp.float32),
            pltpu.VMEM((tasks, LANES), jnp.float32),
            pltpu.VMEM((tasks, LANES), jnp.float32),
            pltpu.VMEM((rows, width), jnp.float32),
            pltpu.SemaphoreType.DMA((pl.cdiv(width, 256),)),
        ],
        compiler_params=params(8),
        cost_estimate=pl.CostEstimate(
            flops=2 * rows * tokens * width, bytes_accessed=4 * rows * width, transcendentals=0
        ),
        name="finish",
    )(order, grams, *mine, *other, acts_rows)


def moved(value, axis, offset):
    count = lax.axis_size(axis)
    return lax.ppermute(value, axis, [((i + offset) % count, i) for i in range(count)])


def shards(acts, out_grads, order):
    tasks = lax.axis_size(TASK)
    task = lax.axis_index(TASK)
    part_rows = acts.shape[1] // tasks
    own = out_grads[0]
    mine = [own] + [moved(own, "task_0", offset) for offset in (1, 2, 3)]
    other = [moved(block, "task_1", 1) for block in mine]
    outer = lax.dot_general(acts, acts, (((1,), (1,)), ((), ())), preferred_element_type=jnp.float32)
    acts_rows = lax.dynamic_slice_in_dim(acts, task * part_rows, part_rows, 1).T
    row = partial_gram(mine, other, outer, lax.axis_size(PARAM))
    row, acts_rows = lax.optimization_barrier((row, acts_rows))
    grams = lax.all_to_all(row, PARAM, 0, 0, tiled=True)
    return finish(order, grams, mine, other, acts_rows)


def solution(mesh):
    split = Mesh(mesh.devices.reshape(4, 2, 4, 4), ("task_0", "task_1", "param_0", "param_1"))
    placed = (P(), P(TASK, None, PARAM), P())
    return jax.shard_map(
        shards, mesh=split, in_specs=placed, out_specs=(P(TASK, PARAM), P()), check_vma=False
    )
```

time: 40.7 us -> 34.1 us (0.84)
  waiting for transfers between devices: 9.09 us -> 6.62 us
  local copies, waits for them, and re-layouts: 2.47 us -> 0.26 us
  starting transfers between devices: 8.05 us -> 6.35 us
  Pallas kernels: 4.67 us -> 4.17 us
    all_to_all x1 -> x0, starting transfers between devices: 8.05 us -> none  [from_everyone(): lax.all_to_all(jnp.broadcast_to(value[None], (devices, *value.shape)), ax...]
    all_to_all x1 -> x0, waiting for transfers between devices: 7.41 us -> none  [from_everyone(): lax.all_to_all(jnp.broadcast_to(value[None], (devices, *value.shape)), ax...]
    ppermute x1 -> x7, starting transfers between devices: 0.01 us -> 6.35 us  [moved(): lax.ppermute(value, axis, [((i + offset) % count, i) for i in range(count)])]
    ppermute x1 -> x7, waiting for transfers between devices: 1.68 us -> 6.62 us  [moved(): lax.ppermute(value, axis, [((i + offset) % count, i) for i in range(count)])]
    broadcast_in_dim x2 -> x0, local copies, waits for them, and re-layouts: 1.69 us -> none  [from_everyone(): jnp.broadcast_to(value[None], (devices, *value.shape))]
    pallas_call x1, Pallas kernels: 2.48 us -> 1.44 us  [partial_gram(): pl.pallas_call(gram_kernel, out_shape=jax.ShapeDtypeStruct((copies, LANES...]
    pallas_call x1, Pallas kernels: 2.18 us -> 2.73 us  [finish(): pl.pallas_call(finish_kernel, out_shape=(jax.ShapeDtypeStruct((rows, widt...]
    squeeze x1 -> x0, local copies, waits for them, and re-layouts: 0.51 us -> none  [shards(): return (update, weights[0, :groups])]
  transfers between devices with their start and end apart: 2 -> 7, of which waited for: 2 -> 4; matrix products, arithmetic and copies ran while one was open for 2% -> 2% of each run, Pallas kernels for 0% -> 0%
where the time goes in v2:
time: 34.1 us; the launch traced here: 33.9 us
  blocking collectives  15.4 us (45%)
  waiting for transfers between devices  6.62 us (19%)
  starting transfers between devices  6.35 us (19%)
  Pallas kernels  4.17 us (12%)
  between operations  0.69 us (2%)
  matrix products  0.4 us (1%)
    all_to_all x1, blocking collectives, shards(): grams = lax.all_to_all(row, PARAM, 0, 0, tiled=True)  15.4 us
    ppermute x7, waiting for transfers between devices, moved(): lax.ppermute(value, axis, [((i + offset) % count, i) for i in range(count)])  6.62 us
    ppermute x7, starting transfers between devices, moved(): lax.ppermute(value, axis, [((i + offset) % count, i) for i in range(count)])  6.35 us
    pallas_call x1, Pallas kernels, finish(): pl.pallas_call(finish_kernel, out_shape=(jax.ShapeDtypeStruct((rows, widt...  2.73 us
    pallas_call x1, Pallas kernels, partial_gram(): pl.pallas_call(gram_kernel, out_shape=jax.ShapeDtypeStruct((copies, LANES...  1.44 us
  transfers between devices with their start and end apart: 7, of which 4 were waited for; matrix products, arithmetic and copies ran while one was open for 2% of the time, Pallas kernels for 0%

profile of v2, /device:TPU:0, one launch (start us, length us, event | category | flops | bytes accessed | tf_op | source)
XLA Modules:
  0.0 33.9 jit_solution(16383008726259443904)
XLA Ops:
  0.6 0.0 copy-start
  0.6 1.7 %collective-permute-start.2 = (bf16[128,640]{1,0:T(8,128)(2,1)}, bf16[128,640]{1,0:T(8,128)(2,1)S(1)}, u32[]{:S(2)}, u32[]{:S(2)}) collective-permute-start(bf16[128,640]{1,0:T(8,128)(2,1)} %bitcast.9), channel_id=1, source_target_pairs={{96,0},{0,32},{32,64},{64,96},{97,1},{1,33},{33,65},{65,97},{98,2}... | collective-permute-start | bytes 491528 | tf_op jit(solution)/shard_map/ppermute | solution.py:163
  2.3 2.7 %collective-permute-start.1 = (bf16[128,640]{1,0:T(8,128)(2,1)}, bf16[128,640]{1,0:T(8,128)(2,1)S(1)}, u32[]{:S(2)}, u32[]{:S(2)}) collective-permute-start(bf16[128,640]{1,0:T(8,128)(2,1)} %bitcast.10), channel_id=1, source_target_pairs={{64,0},{96,32},{0,64},{32,96},{65,1},{97,33},{1,65},{33,97},{66,2}... | collective-permute-start | bytes 491528 | tf_op jit(solution)/shard_map/ppermute | solution.py:163
  5.0 1.4 %collective-permute-start = (bf16[128,640]{1,0:T(8,128)(2,1)}, bf16[128,640]{1,0:T(8,128)(2,1)S(1)}, u32[]{:S(2)}, u32[]{:S(2)}) collective-permute-start(bf16[128,640]{1,0:T(8,128)(2,1)} %bitcast.11), channel_id=1, source_target_pairs={{32,0},{64,32},{96,64},{0,96},{33,1},{65,33},{97,65},{1,97},{34,2}... | collective-permute-start | bytes 491528 | tf_op jit(solution)/shard_map/ppermute | solution.py:163
  6.5 0.0 collective-permute-start.3
  6.5 0.0 copy-done
  6.5 0.0 copy-start.1
  6.5 0.1 constant_dynamic-slice_fusion
  6.6 0.1 copy.8
  6.7 1.3 %collective-permute-done.2.refs_3_.refs_5_ = bf16[128,640]{1,0:T(8,128)(2,1)S(1)} collective-permute-done((bf16[128,640]{1,0:T(8,128)(2,1)}, bf16[128,640]{1,0:T(8,128)(2,1)S(1)}, u32[]{:S(2)}, u32[]{:S(2)}) %collective-permute-start.2) | collective-permute-done | bytes 163872 | tf_op jit(solution)/shard_map/ppermute | solution.py:163
  8.0 0.0 collective-permute-start.6
  8.0 4.7 %collective-permute-done.1.refs_2_.refs_4_ = bf16[128,640]{1,0:T(8,128)(2,1)S(1)} collective-permute-done((bf16[128,640]{1,0:T(8,128)(2,1)}, bf16[128,640]{1,0:T(8,128)(2,1)S(1)}, u32[]{:S(2)}, u32[]{:S(2)}) %collective-permute-start.1) | collective-permute-done | bytes 163872 | tf_op jit(solution)/shard_map/ppermute | solution.py:163
  12.7 0.0 collective-permute-start.5
  12.7 0.0 collective-permute-done.refs_1_.refs_3_
  12.7 0.5 %collective-permute-start.4 = (bf16[128,640]{1,0:T(8,128)(2,1)S(1)}, bf16[128,640]{1,0:T(8,128)(2,1)S(1)}, u32[]{:S(2)}, u32[]{:S(2)}) collective-permute-start(bf16[128,640]{1,0:T(8,128)(2,1)S(1)} %collective-permute-done.refs_1_.refs_3_), channel_id=1, source_target_pairs={{16,0},{0,16},{17,1},{1,17},{18,2},{2,18},{19,3},{3,19},{20,4},{4,... | collective-permute-start | bytes 491528 | tf_op jit(solution)/shard_map/ppermute | solution.py:163
  13.2 0.4 %fusion.refs_8_ = f32[128,128]{1,0:T(8,128)S(1)} fusion(bf16[128,3584]{1,0:T(8,128)(2,1)S(1)} %copy-done), kind=kOutput, calls=%fused_computation.1 | convolution fusion | flops 117440512 | bytes 983040 | tf_op jit(solution)/shard_map/dot_general | solution.py:173
  13.6 0.0 copy-start.2
  13.6 0.0 collective-permute-done.3.refs_4_.refs_6_
  13.6 0.0 collective-permute-done.6.refs_7_.refs_9_
  13.6 0.4 %collective-permute-done.5.refs_6_.refs_8_ = bf16[128,640]{1,0:T(8,128)(2,1)S(1)} collective-permute-done((bf16[128,640]{1,0:T(8,128)(2,1)S(1)}, bf16[128,640]{1,0:T(8,128)(2,1)S(1)}, u32[]{:S(2)}, u32[]{:S(2)}) %collective-permute-start.5) | collective-permute-done | bytes 163872 | tf_op jit(solution)/shard_map/ppermute | solution.py:163
  14.1 0.2 collective-permute-done.4.refs_5_.refs_7_
  14.3 0.0 copy-done.1
  14.3 1.4 %partial_gram.1 = f32[16,128]{1,0:T(8,128)S(1)} custom-call(bf16[128,640]{1,0:T(8,128)(2,1)S(1)} %bitcast.13, bf16[128,640]{1,0:T(8,128)(2,1)S(1)} %collective-permute-done.refs_1_.refs_3_, bf16[128,640]{1,0:T(8,128)(2,1)S(1)} %collective-permute-done.1.refs_2_.refs_4_, bf16[128,640]{1,0:T(8,128)(2,1)S(1)} %collective-permute-done.2.refs_3_.refs_5_, ...), custom_call_target="tpu_custom_call" | custom-call | flops 671088640 | tf_op jit(solution)/shard_map/partial_gram/pallas_call | solution.py:64
  15.8 15.4 %all_to_all.11 = f32[16,1,128]{2,1,0:T(1,128)S(1)} all-to-all(f32[16,1,128]{2,1,0:T(1,128)S(1)} %bitcast.16), channel_id=1, replica_groups=mesh['task_0'=4,'task_1'=2,'param_0'=4,'param_1'=4] {'param_0','param_1'}, dimensions={0} | all-to-all | bytes 16384 | tf_op jit(solution)/shard_map/all_to_all | solution.py:177
  31.2 0.0 copy-done.2
  31.2 2.7 %finish.1 = (f32[448,640]{1,0:T(8,128)}, f32[8]{0:T(128)}) custom-call(s32[8]{0:T(128)S(1)} %copy-done.2, f32[16,128]{1,0:T(8,128)S(1)} %bitcast.15, bf16[128,640]{1,0:T(8,128)(2,1)S(1)} %bitcast.14, bf16[128,640]{1,0:T(8,128)(2,1)S(1)} %collective-permute-done.refs_1_.refs_3_, bf16[128,640]{1,0:T(8,128)(2,1)S(1)} %collective-permute-done.1.refs_2_.refs_4_, ...), custom_call_target="tpu_custom_call" | custom-call | flops 73400320 | bytes 1146880 | tf_op jit(solution)/shard_map/finish/pallas_call | solution.py:138
Async XLA Ops:
  0.6 5.9 %copy-start = (bf16[128,3584]{1,0:T(8,128)(2,1)S(1)}, bf16[128,3584]{1,0:T(8,128)(2,1)}, u32[]{:S(2)}) copy-start(bf16[128,3584]{1,0:T(8,128)(2,1)} %param.3) | copy-start | bytes 2752516
  0.6 7.3 %collective-permute-start.2 = (bf16[128,640]{1,0:T(8,128)(2,1)}, bf16[128,640]{1,0:T(8,128)(2,1)S(1)}, u32[]{:S(2)}, u32[]{:S(2)}) collective-permute-start(bf16[128,640]{1,0:T(8,128)(2,1)} %bitcast.9), channel_id=1, source_target_pairs={{96,0},{0,32},{32,64},{64,96},{97,1},{1,33},{33,65},{65,97},{98,2}... | collective-permute-start | bytes 491528 | tf_op jit(solution)/shard_map/ppermute | solution.py:163
  2.3 10.4 %collective-permute-start.1 = (bf16[128,640]{1,0:T(8,128)(2,1)}, bf16[128,640]{1,0:T(8,128)(2,1)S(1)}, u32[]{:S(2)}, u32[]{:S(2)}) collective-permute-start(bf16[128,640]{1,0:T(8,128)(2,1)} %bitcast.10), channel_id=1, source_target_pairs={{64,0},{96,32},{0,64},{32,96},{65,1},{97,33},{1,65},{33,97},{66,2}... | collective-permute-start | bytes 491528 | tf_op jit(solution)/shard_map/ppermute | solution.py:163
  5.0 7.6 %collective-permute-start = (bf16[128,640]{1,0:T(8,128)(2,1)}, bf16[128,640]{1,0:T(8,128)(2,1)S(1)}, u32[]{:S(2)}, u32[]{:S(2)}) collective-permute-start(bf16[128,640]{1,0:T(8,128)(2,1)} %bitcast.11), channel_id=1, source_target_pairs={{32,0},{64,32},{96,64},{0,96},{33,1},{65,33},{97,65},{1,97},{34,2}... | collective-permute-start | bytes 491528 | tf_op jit(solution)/shard_map/ppermute | solution.py:163
  6.5 7.1 %collective-permute-start.3 = (bf16[128,640]{1,0:T(8,128)(2,1)}, bf16[128,640]{1,0:T(8,128)(2,1)S(1)}, u32[]{:S(2)}, u32[]{:S(2)}) collective-permute-start(bf16[128,640]{1,0:T(8,128)(2,1)} %bitcast.12), channel_id=1, source_target_pairs={{16,0},{0,16},{17,1},{1,17},{18,2},{2,18},{19,3},{3,19},{20,4},{4,... | collective-permute-start | bytes 491528 | tf_op jit(solution)/shard_map/ppermute | solution.py:163
  6.5 7.8 %copy-start.1 = (bf16[1,128,640]{2,1,0:T(8,128)(2,1)S(1)}, bf16[1,128,640]{2,1,0:T(8,128)(2,1)}, u32[]{:S(2)}) copy-start(bf16[1,128,640]{2,1,0:T(8,128)(2,1)} %param.4) | copy-start | bytes 491524
  8.0 5.6 %collective-permute-start.6 = (bf16[128,640]{1,0:T(8,128)(2,1)S(1)}, bf16[128,640]{1,0:T(8,128)(2,1)S(1)}, u32[]{:S(2)}, u32[]{:S(2)}) collective-permute-start(bf16[128,640]{1,0:T(8,128)(2,1)S(1)} %collective-permute-done.2.refs_3_.refs_5_), channel_id=1, source_target_pairs={{16,0},{0,16},{17,1},{1,17},{18,2},{2,18},{19,3},{3,19},{20,4},{4,... | collective-permute-start | bytes 491528 | tf_op jit(solution)/shard_map/ppermute | solution.py:163
  12.7 1.4 %collective-permute-start.5 = (bf16[128,640]{1,0:T(8,128)(2,1)S(1)}, bf16[128,640]{1,0:T(8,128)(2,1)S(1)}, u32[]{:S(2)}, u32[]{:S(2)}) collective-permute-start(bf16[128,640]{1,0:T(8,128)(2,1)S(1)} %collective-permute-done.1.refs_2_.refs_4_), channel_id=1, source_target_pairs={{16,0},{0,16},{17,1},{1,17},{18,2},{2,18},{19,3},{3,19},{20,4},{4,... | collective-permute-start | bytes 491528 | tf_op jit(solution)/shard_map/ppermute | solution.py:163
  12.7 1.6 %collective-permute-start.4 = (bf16[128,640]{1,0:T(8,128)(2,1)S(1)}, bf16[128,640]{1,0:T(8,128)(2,1)S(1)}, u32[]{:S(2)}, u32[]{:S(2)}) collective-permute-start(bf16[128,640]{1,0:T(8,128)(2,1)S(1)} %collective-permute-done.refs_1_.refs_3_), channel_id=1, source_target_pairs={{16,0},{0,16},{17,1},{1,17},{18,2},{2,18},{19,3},{3,19},{20,4},{4,... | collective-permute-start | bytes 491528 | tf_op jit(solution)/shard_map/ppermute | solution.py:163
  13.6 17.6 %copy-start.2 = (s32[8]{0:T(128)S(1)}, s32[8]{0:T(128)}, u32[]{:S(2)}) copy-start(s32[8]{0:T(128)} %refs_0_.1) | copy-start | bytes 100

commit v3 on v2

v3 whole, which is shorter than its diff:
```python
import jax
import jax.numpy as jnp
from jax import lax
from jax.experimental import pallas as pl
from jax.experimental.pallas import tpu as pltpu
from jax.sharding import Mesh
from jax.sharding import PartitionSpec as P

TASK = ("task_0", "task_1")
PARAM = ("param_0", "param_1")
LANES = 128
VMEM = pl.BlockSpec(memory_space=pltpu.VMEM)


def params(mib):
    return pltpu.CompilerParams(vmem_limit_bytes=mib << 20)


def chip_at(offset, chips):
    return lax.rem(lax.axis_index("task_0") + offset, chips)


def prepare_kernel(
    order_hbm, acts_hbm, own_hbm, outer_ref, rows_ref, turns_ref, own_ref,
    order_ref, acts_ref, both_ref, sems,
):
    copies = [
        pltpu.make_async_copy(acts_hbm, acts_ref, sems.at[0]),
        pltpu.make_async_copy(order_hbm, order_ref, sems.at[1]),
        pltpu.make_async_copy(own_hbm, own_ref, sems.at[2]),
    ]
    for copy in copies:
        copy.start()
    task = lax.axis_index("task_0") * 2 + lax.axis_index("task_1")
    tasks = turns_ref.shape[0]
    span = both_ref.shape[0]
    count = rows_ref.shape[0]
    base = (task // 2) * span
    copies[0].wait()
    outer_ref[...] = lax.dot_general(
        acts_ref[...], acts_ref[...], (((1,), (1,)), ((), ())), preferred_element_type=jnp.float32
    )
    for at in range(0, span, LANES):
        part = acts_ref[:, pl.ds(pl.multiple_of(base + at, LANES), LANES)]
        both_ref[at : at + LANES] = part.T
    rows_ref[...] = both_ref[pl.ds(pl.multiple_of((task % 2) * count, 64), count)]
    copies[1].wait()
    for step in range(tasks):
        turns_ref[step] = jnp.full((tasks, LANES), order_ref[step], jnp.int32)
    copies[2].wait()


def prepare(order, acts, own):
    tokens, depth = acts.shape
    tasks = order.shape[0]
    rows = depth // tasks
    return pl.pallas_call(
        prepare_kernel,
        out_shape=(
            jax.ShapeDtypeStruct((tokens, tokens), jnp.float32),
            jax.ShapeDtypeStruct((rows, tokens), acts.dtype),
            jax.ShapeDtypeStruct((tasks, tasks, LANES), jnp.int32),
            jax.ShapeDtypeStruct(own.shape, own.dtype),
        ),
        in_specs=[pl.BlockSpec(memory_space=pltpu.HBM)] * 3,
        out_specs=(VMEM,) * 4,
        scratch_shapes=[
            pltpu.SMEM((tasks,), jnp.int32),
            pltpu.VMEM(acts.shape, acts.dtype),
            pltpu.VMEM((2 * rows, tokens), acts.dtype),
            pltpu.SemaphoreType.DMA((3,)),
        ],
        compiler_params=params(8),
        cost_estimate=pl.CostEstimate(
            flops=2 * tokens * tokens * depth, bytes_accessed=0, transcendentals=0
        ),
        name="prepare",
    )(order, acts, own)


def place(flat_ref, offset, chips, mine_ref, other_ref):
    core = lax.axis_index("task_1")
    base = chip_at(offset, chips) * 2
    flat_ref[base + core] = mine_ref[...]
    flat_ref[base + 1 - core] = other_ref[...]


def chip_pair(flat_ref, rows_ref, outer, chips, first, second):
    tokens = outer.shape[0]
    first_chip, second_chip = chip_at(first, chips), chip_at(second, chips)
    low = 2 * jnp.minimum(first_chip, second_chip)
    high = 2 * jnp.maximum(first_chip, second_chip)
    block = lax.dot_general(
        flat_ref[pl.ds(low, 2)].reshape(2 * tokens, -1), flat_ref[pl.ds(high, 2)].reshape(2 * tokens, -1),
        (((1,), (1,)), ((), ())), preferred_element_type=jnp.float32,
    )
    for a in range(2):
        for b in range(2):
            if first == second and b < a:
                continue
            pair = block[tokens * a : tokens * (a + 1), tokens * b : tokens * (b + 1)]
            row = jnp.sum(pair * outer, axis=0, keepdims=True)
            rows_ref[high + b, pl.ds(low + a, 1), :] = row
            if first != second or a != b:
                rows_ref[low + a, pl.ds(high + b, 1), :] = row


def early_kernel(m0, m1, m3, o0, o1, o3, outer_ref, flat_ref, rows_ref):
    chips = flat_ref.shape[0] // 2
    for offset, mine_ref, other_ref in ((0, m0, o0), (1, m1, o1), (3, m3, o3)):
        place(flat_ref, offset, chips, mine_ref, other_ref)
    outer = outer_ref[...]
    for first, second in ((0, 0), (1, 1), (3, 3), (0, 1), (0, 3), (1, 3)):
        chip_pair(flat_ref, rows_ref, outer, chips, first, second)


def late_kernel(flat_in_ref, rows_in_ref, m2, o2, outer_ref, row_ref, flat_ref, rows_ref):
    chips = flat_ref.shape[0] // 2
    tasks = 2 * chips
    place(flat_ref, 2, chips, m2, o2)
    outer = outer_ref[...]
    for offset in (2, 0, 1, 3):
        chip_pair(flat_ref, rows_ref, outer, chips, 2, offset)
    lane = lax.broadcasted_iota(jnp.int32, (tasks, LANES), 1)
    sub = lax.broadcasted_iota(jnp.int32, (tasks, LANES), 0)
    gram = jnp.zeros((tasks, LANES), jnp.float32)
    for j in range(tasks):
        total = jnp.sum(rows_ref[j], axis=1, keepdims=True)
        gram = jnp.where(lane == tasks * sub + j, total, gram)
    row_ref[...] = jnp.broadcast_to(jnp.sum(gram, axis=0, keepdims=True), row_ref.shape)


def partial_gram(mine, other, outer, copies):
    tokens, width = mine[0].shape
    tasks = 2 * len(mine)
    pair_flops = 8 * tokens * tokens * width
    held = (
        jax.ShapeDtypeStruct((tasks, tokens, width), jnp.bfloat16),
        jax.ShapeDtypeStruct((tasks, tasks, LANES), jnp.float32),
    )
    flat, rows = pl.pallas_call(
        early_kernel,
        out_shape=held,
        in_specs=[VMEM] * 7,
        out_specs=(VMEM, VMEM),
        compiler_params=params(8),
        cost_estimate=pl.CostEstimate(flops=6 * pair_flops, bytes_accessed=0, transcendentals=0),
        name="early_gram",
    )(mine[0], mine[1], mine[3], other[0], other[1], other[3], outer)
    row, _, _ = pl.pallas_call(
        late_kernel,
        out_shape=(jax.ShapeDtypeStruct((copies, LANES), jnp.float32), *held),
        in_specs=[VMEM] * 5,
        out_specs=(VMEM, VMEM, VMEM),
        input_output_aliases={0: 1, 1: 2},
        compiler_params=params(8),
        cost_estimate=pl.CostEstimate(flops=4 * pair_flops, bytes_accessed=0, transcendentals=0),
        name="late_gram",
    )(flat, rows, mine[2], other[2], outer)
    return row


def finish_kernel(*refs):
    chips = (len(refs) - 9) // 2
    turns_ref, grams_ref = refs[:2]
    mine, other = refs[2 : 2 + chips], refs[2 + chips : 2 + 2 * chips]
    acts_ref, update_ref, weights_ref, spread_ref, flat_ref, out_ref, sems = refs[-7:]
    core = lax.axis_index("task_1")
    _, width = mine[0].shape
    tasks = 2 * chips
    lane = lax.broadcasted_iota(jnp.int32, (tasks, LANES), 1)
    sub = lax.broadcasted_iota(jnp.int32, (tasks, LANES), 0)
    column_of = lane - tasks * sub
    gram = jnp.sum(grams_ref[...], axis=0, keepdims=True)
    gram = jnp.broadcast_to(gram, (tasks, LANES))
    mix = (lane == sub).astype(jnp.float32)
    steps = []
    for step in range(tasks):
        target = turns_ref[step]
        column = jnp.sum(jnp.where(column_of == target, gram, 0.0), axis=1, keepdims=True)
        column = jnp.broadcast_to(column, (tasks, LANES))
        scale = jnp.sum(jnp.where(sub == target, column, 0.0), axis=0, keepdims=True) + 1e-06
        steps.append((column, 1.0 / scale, (sub == target) & (lane != target)))
    for column, factor, touched in steps:
        dots = jnp.sum(mix * column, axis=0, keepdims=True)
        change = jnp.minimum(dots, 0.0) * factor
        mix = mix - jnp.where(touched, change, 0.0)
    weights = jnp.sum(jnp.where(lane < tasks, mix, 0.0), axis=1, keepdims=True)
    spread = jnp.broadcast_to(weights, (tasks, LANES))
    spread_ref[...] = spread
    flat_ref[...] = jnp.sum(jnp.where(lane == sub, spread, 0.0), axis=0)[:tasks]
    copies = [pltpu.make_async_copy(flat_ref, weights_ref, sems.at[0])]
    copies[0].start()
    terms = []
    for offset in range(chips):
        base = chip_at(offset, chips) * 2
        terms.append((spread_ref[pl.ds(base + core, 1), :], mine[offset]))
        terms.append((spread_ref[pl.ds(base + 1 - core, 1), :], other[offset]))
    for start in range(0, width, 256):
        size = min(256, width - start)
        blocks = []
        for at in range(start, start + size, LANES):
            total = None
            for factor, ref in terms:
                part = factor * ref[:, at : at + LANES].astype(jnp.float32)
                total = part if total is None else total + part
            blocks.append(total.astype(jnp.bfloat16))
        cols = pl.ds(start, size)
        out_ref[:, cols] = lax.dot_general(
            acts_ref[...], jnp.concatenate(blocks, axis=1), (((1,), (0,)), ((), ())),
            preferred_element_type=jnp.float32,
        )
        copy = pltpu.make_async_copy(out_ref.at[:, cols], update_ref.at[:, cols], sems.at[len(copies)])
        copy.start()
        copies.append(copy)
    for copy in copies:
        copy.wait()


def finish(turns, grams, mine, other, acts_rows):
    tokens, width = mine[0].shape
    tasks = 2 * len(mine)
    rows = acts_rows.shape[0]
    return pl.pallas_call(
        finish_kernel,
        out_shape=(
            jax.ShapeDtypeStruct((rows, width), jnp.float32),
            jax.ShapeDtypeStruct((tasks,), jnp.float32),
        ),
        in_specs=[VMEM] * (tasks + 3),
        out_specs=(pl.BlockSpec(memory_space=pl.ANY),) * 2,
        scratch_shapes=[
            pltpu.VMEM((tasks, LANES), jnp.float32),
            pltpu.VMEM((tasks,), jnp.float32),
            pltpu.VMEM((rows, width), jnp.float32),
            pltpu.SemaphoreType.DMA((1 + pl.cdiv(width, 256),)),
        ],
        compiler_params=params(8),
        cost_estimate=pl.CostEstimate(
            flops=2 * rows * tokens * width, bytes_accessed=4 * rows * width, transcendentals=0
        ),
        name="finish",
    )(turns, grams, *mine, *other, acts_rows)


def moved(value, axis, offset):
    count = lax.axis_size(axis)
    return lax.ppermute(value, axis, [((i + offset) % count, i) for i in range(count)])


def shards(acts, out_grads, order):
    mine, other = [out_grads[0]], []
    for offset in (1, 2, 3):
        mine.append(moved(mine[0], "task_0", offset))
    for offset in (0, 1, 2, 3):
        other.append(moved(mine[offset], "task_1", 1))
    outer, acts_rows, turns, held = prepare(order, acts, mine[0])
    mine[0] = held
    row = partial_gram(mine, other, outer, lax.axis_size(PARAM))
    grams = lax.all_to_all(row, PARAM, 0, 0, tiled=True)
    return finish(turns, grams, mine, other, acts_rows)


def solution(mesh):
    split = Mesh(mesh.devices.reshape(4, 2, 4, 4), ("task_0", "task_1", "param_0", "param_1"))
    placed = (P(), P(TASK, None, PARAM), P())
    return jax.shard_map(
        shards, mesh=split, in_specs=placed, out_specs=(P(TASK, PARAM), P()), check_vma=False
    )
```

time: 34.1 us -> 35.4 us (1.038)
  local copies, waits for them, and re-layouts: 0.26 us -> 2.75 us
  starting transfers between devices: 6.35 us -> 5.24 us
  matrix products: 0.4 us -> 0 us
    unnamed x7 -> x6, local copies, waits for them, and re-layouts: 0.16 us -> 2.75 us
    pallas_call x1 -> x3, Pallas kernels: 1.44 us -> 2.56 us  [the longest x1 0.92 us: partial_gram(): pl.pallas_call(early_kernel, out_shape=held, in_specs=[VMEM] * 7, out_spe...]
    ppermute x7, starting transfers between devices: 6.35 us -> 5.24 us  [moved(): lax.ppermute(value, axis, [((i + offset) % count, i) for i in range(count)])]
    pallas_call x1, Pallas kernels: 2.73 us -> 1.68 us  [finish(): pl.pallas_call(finish_kernel, out_shape=(jax.ShapeDtypeStruct((rows, widt...]
    dot_general x1 -> x0, matrix products: 0.4 us -> none  [shards(): lax.dot_general(acts, acts, (((1,), (1,)), ((), ())), preferred_element_t...]
  transfers between devices with their start and end apart: 7 -> 7, of which waited for: 4 -> 3; matrix products, arithmetic and copies ran while one was open for 2% -> 0% of each run, Pallas kernels for 0% -> 5%
where the time goes in v3:
time: 35.4 us; the launch traced here: 35.2 us
  blocking collectives  15.4 us (44%)
  waiting for transfers between devices  6.81 us (19%)
  starting transfers between devices  5.24 us (15%)
  Pallas kernels  4.25 us (12%)
  local copies, waits for them, and re-layouts  2.75 us (8%)
  between operations  0.69 us (2%)
    all_to_all x1, blocking collectives, shards(): grams = lax.all_to_all(row, PARAM, 0, 0, tiled=True)  15.4 us
    ppermute x7, waiting for transfers between devices, moved(): lax.ppermute(value, axis, [((i + offset) % count, i) for i in range(count)])  6.81 us
    ppermute x7, starting transfers between devices, moved(): lax.ppermute(value, axis, [((i + offset) % count, i) for i in range(count)])  5.24 us
    unnamed x6, local copies, waits for them, and re-layouts  2.75 us
    pallas_call x1, Pallas kernels, finish(): pl.pallas_call(finish_kernel, out_shape=(jax.ShapeDtypeStruct((rows, widt...  1.68 us
    pallas_call x1, Pallas kernels, partial_gram(): pl.pallas_call(early_kernel, out_shape=held, in_specs=[VMEM] * 7, out_spe...  0.92 us
    pallas_call x1, Pallas kernels, prepare(): pl.pallas_call(prepare_kernel, out_shape=(jax.ShapeDtypeStruct((tokens, t...  0.89 us
    pallas_call x1, Pallas kernels, partial_gram(): pl.pallas_call(late_kernel, out_shape=(jax.ShapeDtypeStruct((copies, LANE...  0.75 us
  transfers between devices with their start and end apart: 7, of which 3 were waited for; matrix products, arithmetic and copies ran while one was open for 0% of the time, Pallas kernels for 5%

profile of v3, /device:TPU:0, one launch (start us, length us, event | category | flops | bytes accessed | tf_op | source)
XLA Modules:
  0.0 35.2 jit_solution(9931170810997189202)
XLA Ops:
  0.6 1.7 %collective-permute-start.1 = (bf16[128,640]{1,0:T(8,128)(2,1)}, bf16[128,640]{1,0:T(8,128)(2,1)S(1)}, u32[]{:S(2)}, u32[]{:S(2)}) collective-permute-start(bf16[128,640]{1,0:T(8,128)(2,1)} %bitcast.5), channel_id=1, source_target_pairs={{96,0},{0,32},{32,64},{64,96},{97,1},{1,33},{33,65},{65,97},{98,2}... | collective-permute-start | bytes 491528 | tf_op jit(solution)/shard_map/ppermute | solution.py:248
  2.3 1.6 %collective-permute-start = (bf16[128,640]{1,0:T(8,128)(2,1)}, bf16[128,640]{1,0:T(8,128)(2,1)S(1)}, u32[]{:S(2)}, u32[]{:S(2)}) collective-permute-start(bf16[128,640]{1,0:T(8,128)(2,1)} %bitcast.6), channel_id=1, source_target_pairs={{32,0},{64,32},{96,64},{0,96},{33,1},{65,33},{97,65},{1,97},{34,2}... | collective-permute-start | bytes 491528 | tf_op jit(solution)/shard_map/ppermute | solution.py:248
  3.9 1.9 %collective-permute-start.5 = (bf16[128,640]{1,0:T(8,128)(2,1)}, bf16[128,640]{1,0:T(8,128)(2,1)S(1)}, u32[]{:S(2)}, u32[]{:S(2)}) collective-permute-start(bf16[128,640]{1,0:T(8,128)(2,1)} %bitcast.7), channel_id=1, source_target_pairs={{64,0},{96,32},{0,64},{32,96},{65,1},{97,33},{1,65},{33,97},{66,2}... | collective-permute-start | bytes 491528 | tf_op jit(solution)/shard_map/ppermute | solution.py:248
  5.9 0.0 collective-permute-start.2
  5.9 2.1 %collective-permute-done.1.m3.refs_5_ = bf16[128,640]{1,0:T(8,128)(2,1)S(1)} collective-permute-done((bf16[128,640]{1,0:T(8,128)(2,1)}, bf16[128,640]{1,0:T(8,128)(2,1)S(1)}, u32[]{:S(2)}, u32[]{:S(2)}) %collective-permute-start.1) | collective-permute-done | bytes 163872 | tf_op jit(solution)/shard_map/ppermute | solution.py:248
  8.0 0.0 collective-permute-start.4
  8.0 1.6 %collective-permute-done.m1.refs_3_ = bf16[128,640]{1,0:T(8,128)(2,1)S(1)} collective-permute-done((bf16[128,640]{1,0:T(8,128)(2,1)}, bf16[128,640]{1,0:T(8,128)(2,1)S(1)}, u32[]{:S(2)}, u32[]{:S(2)}) %collective-permute-start) | collective-permute-done | bytes 163872 | tf_op jit(solution)/shard_map/ppermute | solution.py:248
  9.6 0.0 collective-permute-start.3
  9.6 3.1 %collective-permute-done.5.m2.refs_4_ = bf16[128,640]{1,0:T(8,128)(2,1)S(1)} collective-permute-done((bf16[128,640]{1,0:T(8,128)(2,1)}, bf16[128,640]{1,0:T(8,128)(2,1)S(1)}, u32[]{:S(2)}, u32[]{:S(2)}) %collective-permute-start.5) | collective-permute-done | bytes 163872 | tf_op jit(solution)/shard_map/ppermute | solution.py:248
  12.7 0.0 collective-permute-start.6
  12.7 0.0 copy-start
  12.7 1.2 %copy-done = bf16[128,3584]{1,0:T(8,128)(2,1)S(1)} copy-done((bf16[128,3584]{1,0:T(8,128)(2,1)S(1)}, bf16[128,3584]{1,0:T(8,128)(2,1)}, u32[]{:S(2)}) %copy-start) | copy-done | bytes 917528
  13.8 0.0 copy-start.1
  13.9 0.9 %copy-done.1 = bf16[1,128,640]{2,1,0:T(8,128)(2,1)S(1)} copy-done((bf16[1,128,640]{2,1,0:T(8,128)(2,1)S(1)}, bf16[1,128,640]{2,1,0:T(8,128)(2,1)}, u32[]{:S(2)}) %copy-start.1) | copy-done | bytes 163864
  14.8 0.0 copy-start.2
  14.8 0.7 %copy-done.2 = s32[8]{0:T(128)S(1)} copy-done((s32[8]{0:T(128)S(1)}, s32[8]{0:T(128)}, u32[]{:S(2)}) %copy-start.2) | copy-done | bytes 56
  15.4 0.9 %prepare.1 = (f32[128,128]{1,0:T(8,128)S(1)}, bf16[448,128]{1,0:T(8,128)(2,1)S(1)}, s32[8,8,128]{2,1,0:T(8,128)S(1)}, bf16[128,640]{1,0:T(8,128)(2,1)S(1)}) custom-call(s32[8]{0:T(128)S(1)} %copy-done.2, bf16[128,3584]{1,0:T(8,128)(2,1)S(1)} %copy-done, bf16[128,640]{1,0:T(8,128)(2,1)S(1)} %bitcast.9), custom_call_target="tpu_custom_call" | custom-call | flops 117440512 | tf_op jit(solution)/shard_map/prepare/pallas_call | solution.py:57
  16.3 0.0 collective-permute-done.2.o0.refs_6_
  16.3 0.0 collective-permute-done.4.o3.refs_9_
  16.3 0.0 collective-permute-done.3.o1.refs_7_
  16.4 0.9 %early_gram.1 = (bf16[8,128,640]{2,1,0:T(8,128)(2,1)S(1)}, f32[8,8,128]{2,1,0:T(8,128)S(1)}) custom-call(bf16[128,640]{1,0:T(8,128)(2,1)S(1)} %get-tuple-element.10.m0.refs_2_, bf16[128,640]{1,0:T(8,128)(2,1)S(1)} %collective-permute-done.m1.refs_3_, bf16[128,640]{1,0:T(8,128)(2,1)S(1)} %collective-permute-done.1.m3.refs_5_, ...), custom_call_target="tpu_custom_call" | custom-call | flops 503316480 | tf_op jit(solution)/shard_map/early_gram/pallas_call | solution.py:141
  17.3 0.0 collective-permute-done.6.o2.refs_8_
  17.3 0.8 %late_gram.1 = (f32[16,128]{1,0:T(8,128)S(1)}, bf16[8,128,640]{2,1,0:T(8,128)(2,1)S(1)}, f32[8,8,128]{2,1,0:T(8,128)S(1)}) custom-call(bf16[8,128,640]{2,1,0:T(8,128)(2,1)S(1)} %get-tuple-element.12.flat_in_ref, f32[8,8,128]{2,1,0:T(8,128)S(1)} %get-tuple-element.13.rows_in_ref, ...), custom_call_target="tpu_custom_call", output_to_operand_aliasing={{1}: (0, {}), {2}: (1, {})} | custom-call | flops 335544320 | tf_op jit(solution)/shard_map/late_gram/pallas_call | solution.py:150
  18.0 15.4 %all_to_all.11 = f32[16,1,128]{2,1,0:T(1,128)S(1)} all-to-all(f32[16,1,128]{2,1,0:T(1,128)S(1)} %bitcast.11), channel_id=1, replica_groups=mesh['task_0'=4,'task_1'=2,'param_0'=4,'param_1'=4] {'param_0','param_1'}, dimensions={0} | all-to-all | bytes 16384 | tf_op jit(solution)/shard_map/all_to_all | solution.py:260
  33.5 1.7 %finish.1 = (f32[448,640]{1,0:T(8,128)}, f32[8]{0:T(128)}) custom-call(s32[8,8,128]{2,1,0:T(8,128)S(1)} %get-tuple-element.9.refs_0_, f32[16,128]{1,0:T(8,128)S(1)} %bitcast.10, bf16[128,640]{1,0:T(8,128)(2,1)S(1)} %get-tuple-element.10.m0.refs_2_, bf16[128,640]{1,0:T(8,128)(2,1)S(1)} %collective-permute-done.m1.refs_3_, ...), custom_call_target="tpu_custom_call" | custom-call | flops 73400320 | bytes 1146880 | tf_op jit(solution)/shard_map/finish/pallas_call | solution.py:224
Async XLA Ops:
  0.6 7.3 %collective-permute-start.1 = (bf16[128,640]{1,0:T(8,128)(2,1)}, bf16[128,640]{1,0:T(8,128)(2,1)S(1)}, u32[]{:S(2)}, u32[]{:S(2)}) collective-permute-start(bf16[128,640]{1,0:T(8,128)(2,1)} %bitcast.5), channel_id=1, source_target_pairs={{96,0},{0,32},{32,64},{64,96},{97,1},{1,33},{33,65},{65,97},{98,2}... | collective-permute-start | bytes 491528 | tf_op jit(solution)/shard_map/ppermute | solution.py:248
  2.3 7.3 %collective-permute-start = (bf16[128,640]{1,0:T(8,128)(2,1)}, bf16[128,640]{1,0:T(8,128)(2,1)S(1)}, u32[]{:S(2)}, u32[]{:S(2)}) collective-permute-start(bf16[128,640]{1,0:T(8,128)(2,1)} %bitcast.6), channel_id=1, source_target_pairs={{32,0},{64,32},{96,64},{0,96},{33,1},{65,33},{97,65},{1,97},{34,2}... | collective-permute-start | bytes 491528 | tf_op jit(solution)/shard_map/ppermute | solution.py:248
  3.9 8.7 %collective-permute-start.5 = (bf16[128,640]{1,0:T(8,128)(2,1)}, bf16[128,640]{1,0:T(8,128)(2,1)S(1)}, u32[]{:S(2)}, u32[]{:S(2)}) collective-permute-start(bf16[128,640]{1,0:T(8,128)(2,1)} %bitcast.7), channel_id=1, source_target_pairs={{64,0},{96,32},{0,64},{32,96},{65,1},{97,33},{1,65},{33,97},{66,2}... | collective-permute-start | bytes 491528 | tf_op jit(solution)/shard_map/ppermute | solution.py:248
  5.9 10.5 %collective-permute-start.2 = (bf16[128,640]{1,0:T(8,128)(2,1)}, bf16[128,640]{1,0:T(8,128)(2,1)S(1)}, u32[]{:S(2)}, u32[]{:S(2)}) collective-permute-start(bf16[128,640]{1,0:T(8,128)(2,1)} %bitcast.8), channel_id=1, source_target_pairs={{16,0},{0,16},{17,1},{1,17},{18,2},{2,18},{19,3},{3,19},{20,4},{4,... | collective-permute-start | bytes 491528 | tf_op jit(solution)/shard_map/ppermute | solution.py:248
  8.0 8.4 %collective-permute-start.4 = (bf16[128,640]{1,0:T(8,128)(2,1)S(1)}, bf16[128,640]{1,0:T(8,128)(2,1)S(1)}, u32[]{:S(2)}, u32[]{:S(2)}) collective-permute-start(bf16[128,640]{1,0:T(8,128)(2,1)S(1)} %collective-permute-done.1.m3.refs_5_), channel_id=1, source_target_pairs={{16,0},{0,16},{17,1},{1,17},{18,2},{2,18},{19,3},{3,19},{20,4},{4,... | collective-permute-start | bytes 491528 | tf_op jit(solution)/shard_map/ppermute | solution.py:248
  9.6 6.8 %collective-permute-start.3 = (bf16[128,640]{1,0:T(8,128)(2,1)S(1)}, bf16[128,640]{1,0:T(8,128)(2,1)S(1)}, u32[]{:S(2)}, u32[]{:S(2)}) collective-permute-start(bf16[128,640]{1,0:T(8,128)(2,1)S(1)} %collective-permute-done.m1.refs_3_), channel_id=1, source_target_pairs={{16,0},{0,16},{17,1},{1,17},{18,2},{2,18},{19,3},{3,19},{20,4},{4,... | collective-permute-start | bytes 491528 | tf_op jit(solution)/shard_map/ppermute | solution.py:248
  12.7 4.6 %collective-permute-start.6 = (bf16[128,640]{1,0:T(8,128)(2,1)S(1)}, bf16[128,640]{1,0:T(8,128)(2,1)S(1)}, u32[]{:S(2)}, u32[]{:S(2)}) collective-permute-start(bf16[128,640]{1,0:T(8,128)(2,1)S(1)} %collective-permute-done.5.m2.refs_4_), channel_id=1, source_target_pairs={{16,0},{0,16},{17,1},{1,17},{18,2},{2,18},{19,3},{3,19},{20,4},{4,... | collective-permute-start | bytes 491528 | tf_op jit(solution)/shard_map/ppermute | solution.py:248
  12.7 1.2 %copy-start = (bf16[128,3584]{1,0:T(8,128)(2,1)S(1)}, bf16[128,3584]{1,0:T(8,128)(2,1)}, u32[]{:S(2)}) copy-start(bf16[128,3584]{1,0:T(8,128)(2,1)} %acts_hbm.1) | copy-start | bytes 2752516
  13.8 0.9 %copy-start.1 = (bf16[1,128,640]{2,1,0:T(8,128)(2,1)S(1)}, bf16[1,128,640]{2,1,0:T(8,128)(2,1)}, u32[]{:S(2)}) copy-start(bf16[1,128,640]{2,1,0:T(8,128)(2,1)} %param.4) | copy-start | bytes 491524
  14.8 0.7 %copy-start.2 = (s32[8]{0:T(128)S(1)}, s32[8]{0:T(128)}, u32[]{:S(2)}) copy-start(s32[8]{0:T(128)} %order_hbm.1) | copy-start | bytes 100
